TPU v7x, 32 devices: a whole 2x2x4 slice. The times are simulated.
32 devices in a mesh: row: 4 (over z), col: 4 (over y, core), rep: 2 (over x).
Axes of the slice: x: 2, y: 2, z: 4, core: 2. Of those that a mesh axis runs over, the one named last changes fastest.
Arguments:
- upstream: float32 [16384, 16384], P('row', ('col', 'rep')), may hold values from -0.046875 to 0.046875
- input_panel: float32 [16384, 1024], P('row', ('col', 'rep')), may hold values from -6 to 6
Outputs:
- panel_grad: float32 [16384, 1024], P('row', ('col', 'rep'))
All inputs are finite; a program needn't handle non-finite values.
Results may differ from a plain program's by a relative error of at most 0.000071.
Values sent between devices are 32-bit elements; how exact they have to be, the bound alone decides.
A program may use at most 192 MiB of HBM per device.

v0:
```python
import jax
import jax.numpy as jnp
from jax import lax
from jax.sharding import PartitionSpec as P

GROUP = ("col", "rep")


def product(left, right, contract):
    return lax.dot_general(
        left,
        right,
        (contract, ((), ())),
        precision=lax.Precision.HIGH,
        preferred_element_type=jnp.float32,
    )


def after(value, *first):
    return lax.optimization_barrier((value,) + first)[0]


def rows_up(own, rows):
    me = lax.axis_index("row")
    gathered = jnp.zeros((rows,) + own.shape, own.dtype)
    held = early = own
    for step in range(rows):
        slot = lax.rem(me + rows - step, rows)
        gathered = lax.dynamic_update_slice_in_dim(gathered, held[None], slot, 0)
        if step < rows - 1:
            held = lax.ppermute(held, "row", [(r, r + 1) for r in range(step, rows - 1)])
            if step < rows - 2:
                early = held
    return gathered, early


def rows_down(parts, rows):
    me = lax.axis_index("row")
    arrived = None
    for step in range(1, rows):
        block = jnp.maximum(me + step - rows, 0)
        term = lax.dynamic_index_in_dim(parts, block, 0, keepdims=False)
        total = term if arrived is None else term + arrived
        arrived = lax.ppermute(total, "row", [(r, r - 1) for r in range(rows - step, rows)])
        if step == 1:
            first = arrived
    own = lax.dynamic_index_in_dim(parts, me, 0, keepdims=False)
    if arrived is None:
        return own, own
    return own + arrived, first


def per_device(rows, groups, upstream, input_panel):
    row_count, col_count = upstream.shape
    width = input_panel.shape[1]
    ratio = row_count // col_count
    row_index = lax.axis_index("row")
    col_index = lax.axis_index(GROUP)
    rows_global = row_index * row_count + lax.broadcasted_iota(jnp.int32, (row_count, col_count), 0)
    cols_global = col_index * col_count + lax.broadcasted_iota(jnp.int32, (row_count, col_count), 1)
    lower_tile = jnp.where(cols_global <= rows_global, upstream, jnp.float32(0.0))

    panel_t = jnp.transpose(input_panel)
    band_t = lax.all_gather(panel_t, GROUP, axis=0, tiled=True)
    pieces = jnp.transpose(input_panel.reshape(ratio, col_count, width), (0, 2, 1))
    column_blocks, early = rows_up(pieces, rows)
    column_blocks = column_blocks.reshape(groups, width, col_count)

    upper_t = product(after(band_t, early), lower_tile, ((1,), (0,)))
    upper_blocks = lax.all_to_all(
        upper_t.reshape(groups, width, col_count), GROUP, split_axis=0, concat_axis=0, tiled=True
    )
    upper_total, first = rows_down(upper_blocks.reshape(rows, ratio, width, col_count), rows)

    column_t = lax.all_to_all(
        after(column_blocks, upper_blocks), GROUP, split_axis=0, concat_axis=0, tiled=True
    )
    lower_t = product(after(column_t, first).reshape(groups * width, col_count), lower_tile, ((1,), (1,)))
    lower_total = lax.psum_scatter(lower_t, GROUP, scatter_dimension=0, tiled=True)

    upper_rows = jnp.transpose(upper_total, (0, 2, 1)).reshape(row_count, width)
    return upper_rows + jnp.transpose(lower_total)


def solution(mesh):
    rows = mesh.shape["row"]
    groups = mesh.shape["col"] * mesh.shape["rep"]
    placed = P("row", GROUP)

    def body(upstream, input_panel):
        return per_device(rows, groups, upstream, input_panel)

    return jax.shard_map(
        body, mesh=mesh, in_specs=(placed, placed), out_specs=placed, check_vma=False
    )
```

profile of v0, /device:TPU:13, one launch (start us, length us, event | category | flops | bytes accessed | tf_op | source)
XLA Modules:
  0.0 556.7 jit_solution(15312995943313500061)
XLA Ops:
  6.5 0.0 all-gather.2.cloned.1.call-start
  6.5 0.7 all-gather.2.cloned.1.call-update
  7.3 1.9 copy.8
  9.2 3.2 collective-permute-start
  12.4 45.3 %collective-permute-done = f32[2,128,2048]{2,1,0:T(8,128)} collective-permute-done((f32[2,128,2048]{2,1,0:T(8,128)S(1)}, f32[2,128,2048]{2,1,0:T(8,128)}, u32[]{:S(2)}, u32[]{:S(2)}) %collective-permute-start) | collective-permute-done | bytes 2097184 | tf_op jit(solution)/shard_map/ppermute | solution.py:31
  57.7 4.6 collective-permute-start.1
  62.3 42.4 %collective-permute-done.1 = f32[2,128,2048]{2,1,0:T(8,128)} collective-permute-done((f32[2,128,2048]{2,1,0:T(8,128)}, f32[2,128,2048]{2,1,0:T(8,128)}, u32[]{:S(2)}, u32[]{:S(2)}) %collective-permute-start.1) | collective-permute-done | bytes 2097184 | tf_op jit(solution)/shard_map/ppermute | solution.py:31
  104.7 0.0 all-gather.2.cloned.1.call-done
  104.7 62.6 %fusion.1 = f32[1024,2048]{1,0:T(8,128)} fusion(f32[1024,4096]{0,1:T(8,128)} %all-gather.2.cloned.1.call-done, f32[4096,2048]{1,0:T(8,128)} %param.2, s32[2048]{0:T(1024)S(1)} %iota_add_fusion.1, s32[4096]{0:T(1024)S(1)} %iota_add_fusion), kind=kOutput, calls=%fused_computation.2 | convolution fusion | flops 51556384768 | bytes 58744832 | tf_op jit(solution)/shard_map/dot_general | solution.py:10
  167.3 7.4 %all-to-all-start = ((f32[8,128,2048]{2,1,0:T(8,128)}), f32[8,128,2048]{2,1,0:T(8,128)}, u32[]{:S(2)}, u32[]{:S(2)}) async-start(f32[8,128,2048]{2,1,0:T(8,128)} %bitcast.38), calls=%async_computation | async-start | bytes 16777216 | tf_op jit(solution)/shard_map/all_to_all | solution.py:70
  174.7 2.0 collective-permute-start.5
  176.6 4.3 broadcast_in_dim.20
  180.9 1.5 bitcast_dynamic-update-slice_fusion
  182.4 3.2 bitcast_dynamic-update-slice_fusion.3
  185.6 3.1 bitcast_dynamic-update-slice_fusion.2
  188.7 0.0 collective-permute-done.5
  188.7 3.1 bitcast_dynamic-update-slice_fusion.1
  191.9 75.2 %all-to-all-done = f32[8,128,2048]{2,1,0:T(8,128)} async-done(((f32[8,128,2048]{2,1,0:T(8,128)}), f32[8,128,2048]{2,1,0:T(8,128)}, u32[]{:S(2)}, u32[]{:S(2)}) %all-to-all-start) | async-done | bytes 8388640 | tf_op jit(solution)/shard_map/all_to_all | solution.py:70
  267.0 6.1 %all-to-all-start.1 = ((f32[8,128,2048]{2,1,0:T(8,128)}), f32[8,128,2048]{2,1,0:T(8,128)}, u32[]{:S(2)}, u32[]{:S(2)}) async-start(f32[8,128,2048]{2,1,0:T(8,128)} %bitcast.14), calls=%async_computation.1 | async-start | bytes 16777216 | tf_op jit(solution)/shard_map/all_to_all | solution.py:75
  273.1 0.0 reduce-scatter.2.cloned.1.call-start
  273.1 6.4 %constant_dynamic-slice_fusion.3 = (f32[1,2,128,2048]{3,2,1,0:T(8,128)S(1)}, f32[1,2,128,2048]{3,2,1,0:T(8,128)S(1)}, f32[1,2,128,2048]{3,2,1,0:T(8,128)}, f32[1,2,128,2048]{3,2,1,0:T(8,128)}) fusion(f32[4,2,128,2048]{3,2,1,0:T(8,128)} %bitcast.4, s32[]{:T(128)S(6)} %select_n.24, s32[]{:T(128)S(6)} %max.11, s32[]{:T(128)S(6)} %max.10, s32[]{:T(128)S(6)} %max.9), kind=kLoop, calls=%fused_computation.23 | loop fusion | bytes 16777232 | tf_op jit(solution)/shard_map/jit(dynamic_index_in_dim)/dynamic_slice | solution.py:47
  279.5 1.6 copy.19
  281.1 2.0 collective-permute-start.2
  283.1 0.0 collective-permute-done.2
  283.1 82.4 %all-to-all-done.1 = f32[8,128,2048]{2,1,0:T(8,128)} async-done(((f32[8,128,2048]{2,1,0:T(8,128)}), f32[8,128,2048]{2,1,0:T(8,128)}, u32[]{:S(2)}, u32[]{:S(2)}) %all-to-all-start.1) | async-done | bytes 8388640 | tf_op jit(solution)/shard_map/all_to_all | solution.py:75
  365.5 61.1 %fusion = f32[1024,4096]{1,0:T(8,128)} fusion(f32[1024,2048]{1,0:T(8,128)} %bitcast.15, f32[4096,2048]{1,0:T(8,128)} %param.2, s32[2048]{0:T(1024)S(1)} %iota_add_fusion.1, s32[4096]{0:T(1024)S(1)} %iota_add_fusion), kind=kOutput, calls=%fused_computation.1 | convolution fusion | flops 51556384768 | bytes 58744832 | tf_op jit(solution)/shard_map/dot_general | solution.py:10
  426.6 0.0 reduce-scatter.2.cloned.1.call-update
  426.6 4.4 bitcast_add_fusion.1
  431.0 1.3 collective-permute-start.3
  432.3 48.8 %collective-permute-done.3 = f32[2,128,2048]{2,0,1:T(2,128)S(1)} collective-permute-done((f32[2,128,2048]{2,0,1:T(2,128)S(1)}, f32[2,128,2048]{2,0,1:T(2,128)S(1)}, u32[]{:S(2)}, u32[]{:S(2)}) %collective-permute-start.3) | collective-permute-done | bytes 2097184 | tf_op jit(solution)/shard_map/ppermute | solution.py:44
  481.1 4.0 bitcast_add_fusion.2
  485.1 1.9 collective-permute-start.4
  487.0 46.7 %collective-permute-done.4 = f32[2,128,2048]{2,0,1:T(2,128)S(1)} collective-permute-done((f32[2,128,2048]{2,0,1:T(2,128)S(1)}, f32[2,128,2048]{2,0,1:T(2,128)S(1)}, u32[]{:S(2)}, u32[]{:S(2)}) %collective-permute-start.4) | collective-permute-done | bytes 2097184 | tf_op jit(solution)/shard_map/ppermute | solution.py:44
  533.7 2.2 bitcast_add_fusion.3
  535.9 1.6 copy.14
  537.6 6.3 %reduce-scatter.2.cloned.1.call-done = f32[128,4096]{1,0:T(8,128)} async-done(((f32[1024,4096]{1,0:T(8,128)}), f32[128,4096]{1,0:T(8,128)}) %reduce-scatter.2.cloned.1.call-update) | async-done | bytes 2097168 | tf_op jit(solution)/shard_map/reduce_scatter | solution.py:79
  543.8 3.2 bitcast_add_fusion
  547.0 2.9 copy.13
  (2 shorter events, 0.0 us)
Async XLA Ops:
  6.5 98.1 %all-gather.2.cloned.1.call-start = ((), (), s32[]{:S(2)}) async-start(), calls=%async_computation.3 | async-start | bytes 18874368 | tf_op jit(solution)/shard_map/all_gather | solution.py:64
  9.2 48.5 %collective-permute-start = (f32[2,128,2048]{2,1,0:T(8,128)S(1)}, f32[2,128,2048]{2,1,0:T(8,128)}, u32[]{:S(2)}, u32[]{:S(2)}) collective-permute-start(f32[2,128,2048]{2,1,0:T(8,128)S(1)} %bitcast.41), channel_id=1, source_target_pairs={{0,8},{8,16},{16,24},{1,9},{9,17},{17,25},{2,10},{10,18},{18,26},{... | collective-permute-start | bytes 6291464 | tf_op jit(solution)/shard_map/ppermute | solution.py:31
  57.7 47.0 %collective-permute-start.1 = (f32[2,128,2048]{2,1,0:T(8,128)}, f32[2,128,2048]{2,1,0:T(8,128)}, u32[]{:S(2)}, u32[]{:S(2)}) collective-permute-start(f32[2,128,2048]{2,1,0:T(8,128)} %collective-permute-done), channel_id=1, source_target_pairs={{8,16},{16,24},{9,17},{17,25},{10,18},{18,26},{11,19},{19,27},{12,... | collective-permute-start | bytes 6291464 | tf_op jit(solution)/shard_map/ppermute | solution.py:31
  167.3 99.7 %all-to-all-start = ((f32[8,128,2048]{2,1,0:T(8,128)}), f32[8,128,2048]{2,1,0:T(8,128)}, u32[]{:S(2)}, u32[]{:S(2)}) async-start(f32[8,128,2048]{2,1,0:T(8,128)} %bitcast.38), calls=%async_computation | async-start | bytes 16777216 | tf_op jit(solution)/shard_map/all_to_all | solution.py:70
  174.7 14.1 %collective-permute-start.5 = (f32[2,128,2048]{2,1,0:T(8,128)}, f32[2,128,2048]{2,1,0:T(8,128)}, u32[]{:S(2)}, u32[]{:S(2)}) collective-permute-start(f32[2,128,2048]{2,1,0:T(8,128)} %collective-permute-done.1), channel_id=1, source_target_pairs={{16,24},{17,25},{18,26},{19,27},{20,28},{21,29},{22,30},{23,31}} | collective-permute-start | bytes 6291464 | tf_op jit(solution)/shard_map/ppermute | solution.py:31
  267.0 98.4 %all-to-all-start.1 = ((f32[8,128,2048]{2,1,0:T(8,128)}), f32[8,128,2048]{2,1,0:T(8,128)}, u32[]{:S(2)}, u32[]{:S(2)}) async-start(f32[8,128,2048]{2,1,0:T(8,128)} %bitcast.14), calls=%async_computation.1 | async-start | bytes 16777216 | tf_op jit(solution)/shard_map/all_to_all | solution.py:75
  273.1 270.7 %reduce-scatter.2.cloned.1.call-start = ((), (), s32[]{:S(2)}) async-start(), calls=%async_computation.4 | async-start | bytes 18874368 | tf_op jit(solution)/shard_map/reduce_scatter | solution.py:79
  281.1 2.0 collective-permute-start.2
  431.0 50.1 %collective-permute-start.3 = (f32[2,128,2048]{2,0,1:T(2,128)S(1)}, f32[2,128,2048]{2,0,1:T(2,128)S(1)}, u32[]{:S(2)}, u32[]{:S(2)}) collective-permute-start(f32[2,128,2048]{2,0,1:T(2,128)S(1)} %bitcast_add_fusion.1), channel_id=1, source_target_pairs={{16,8},{24,16},{17,9},{25,17},{18,10},{26,18},{19,11},{27,19},{20,... | collective-permute-start | bytes 6291464 | tf_op jit(solution)/shard_map/ppermute | solution.py:44
  485.1 48.6 %collective-permute-start.4 = (f32[2,128,2048]{2,0,1:T(2,128)S(1)}, f32[2,128,2048]{2,0,1:T(2,128)S(1)}, u32[]{:S(2)}, u32[]{:S(2)}) collective-permute-start(f32[2,128,2048]{2,0,1:T(2,128)S(1)} %bitcast_add_fusion.2), channel_id=1, source_target_pairs={{8,0},{16,8},{24,16},{9,1},{17,9},{25,17},{10,2},{18,10},{26,18},{... | collective-permute-start | bytes 6291464 | tf_op jit(solution)/shard_map/ppermute | solution.py:44
Sparse Core Ops, SparseCore 0:
  9.2 93.6 all-gather.1
  426.7 117.0 reduce-scatter.1
where the time goes:
time: 559 us; the launch traced here: 557 us
  waiting for transfers between devices  348 us (62%)
  matrix products  124 us (22%)
  local copies, waits for them, and re-layouts  29.7 us (5%)
  starting transfers between devices  28.4 us (5%)
  other arithmetic  13.8 us (2%)
  between operations  13.5 us (2%)
    dot_general x2, matrix products, product(): lax.dot_general(left, right, (contract, ((), ())), precision=lax.Precisio...  124 us
    ppermute x3, waiting for transfers between devices, rows_down(): lax.ppermute(total, 'row', [(r, r - 1) for r in range(rows - step, rows)])  95.5 us
    ppermute x3, waiting for transfers between devices, rows_up(): lax.ppermute(held, 'row', [(r, r + 1) for r in range(step, rows - 1)])  87.7 us
    all_to_all x1, waiting for transfers between devices, per_device(): lax.all_to_all(after(column_blocks, upper_blocks), GROUP, split_axis=0, c...  82.4 us
    all_to_all x1, waiting for transfers between devices, per_device(): lax.all_to_all(upper_t.reshape(groups, width, col_count), GROUP, split_ax...  75.2 us
  transfers between devices with their start and end apart: 10, of which 7 were waited for; matrix products, arithmetic and copies ran while one was open for 7% of the time, Pallas kernels for 0%

commit v1 on v0

v1 whole, which is shorter than its diff:
```python
import functools

import jax
import jax.numpy as jnp
from jax import lax
from jax.experimental import pallas as pl
from jax.experimental.pallas import tpu as pltpu
from jax.sharding import PartitionSpec as P

GROUP = ("col", "rep")
ALL = ("row", "col", "rep")
MESH = pl.DeviceIdType.MESH
LANES = 128
CHIPS = 4
OFFSETS = (0, 1, 3, 2)
TILE = 512
DEEP = 256

CHUNKS = 4


def product(left, right, contract):
    return lax.dot_general(
        left,
        right,
        (contract, ((), ())),
        precision=lax.Precision.HIGH,
        preferred_element_type=jnp.float32,
    )


def per_device(rows, groups, upstream, input_panel):
    row_count, col_count = upstream.shape
    width = input_panel.shape[1]
    ratio = row_count // col_count
    row_index = lax.axis_index("row")
    col_index = lax.axis_index(GROUP)
    owner = col_index // ratio
    part = (col_index % ratio) * col_count
    rows_global = row_index * row_count + lax.broadcasted_iota(jnp.int32, (row_count, col_count), 0)
    cols_global = col_index * col_count + lax.broadcasted_iota(jnp.int32, (row_count, col_count), 1)
    lower_tile = jnp.where(cols_global <= rows_global, upstream, jnp.float32(0.0))
    panel_t = jnp.transpose(input_panel)
    step = width // CHUNKS

    def hop(value, pairs):
        return lax.ppermute(value, ALL, [(a * groups + g, b * groups + g) for a, b, g in pairs])

    outs = []
    for c in range(CHUNKS):
        band = lax.all_gather(panel_t[c * step : (c + 1) * step], GROUP, axis=0, tiled=True)
        held = lax.dynamic_slice_in_dim(band, part, col_count, 1)
        block = held
        for s in range(rows - 1):
            pairs = [(g // ratio + s, g // ratio + s + 1, g) for g in range(groups) if g // ratio + s + 1 < rows]
            held = hop(held, pairs)
            block = jnp.where(row_index == owner + s + 1, held, block)
        total = product(band, lower_tile, ((1,), (0,)))
        for s in range(rows - 1):
            r = rows - 1 - s
            pairs = [(r, r - 1, g) for g in range(groups) if g // ratio <= r - 1]
            total = total + hop(total, pairs)
        lower = product(block, lower_tile, ((1,), (1,)))
        total = jnp.where(row_index == owner, total, 0.0)
        here = lax.dynamic_slice_in_dim(lower, part, col_count, 1)
        lower = lax.dynamic_update_slice_in_dim(lower, here + total, part, 1)
        outs.append(lax.psum_scatter(lower, GROUP, scatter_dimension=0, tiled=True))
    return jnp.transpose(jnp.concatenate(outs, 0))


def split(value):
    high = value.astype(jnp.bfloat16)
    low = (value - high.astype(jnp.float32)).astype(jnp.bfloat16)
    return high, low


def dot(left, right):
    return jnp.dot(left, right, preferred_element_type=jnp.float32)


def kernel(rows, upstream, panel, out, ag, pg, uin, rs, uf, cx, t0,
           high, low, work, pt, pgb, u,
           ag_send, ag_recv, pg_send, pg_recv, u_send, u_recv, uf_recv,
           cx_send, cx_recv, rs_send, rs_recv, local):
    full, span = upstream.shape
    ratio = full // span
    r = lax.axis_index("row")
    col = lax.axis_index("col")
    x = lax.axis_index("rep")
    y = col // 2
    core = col % 2
    mate = 1 - core
    g = col * 2 + x
    p = 2 * y + (x + y) % 2
    owner = g // ratio
    part = pl.multiple_of((g % ratio) * span, span)
    active = r >= owner
    last = rows - 1

    def place(chip, c):
        return {"col": 2 * (chip // 2) + c, "rep": (chip + chip // 2) % 2}

    def chip_at(d):
        return lax.rem(p + d, CHIPS)

    def remote(src, dst, send, recv, where):
        return pltpu.make_async_remote_copy(
            src_ref=src, dst_ref=dst, send_sem=send, recv_sem=recv, device_id=where, device_id_type=MESH
        )

    mate_at = place(p, mate)
    above = {"row": jnp.minimum(r + 1, last)}
    below = {"row": jnp.maximum(r - 1, 0)}

    slots = 4
    blocks = span // LANES

    def tile_copy(j, slot):
        columns = pl.ds(pl.multiple_of(j * LANES, LANES), LANES)
        return pltpu.make_async_copy(upstream.at[:, columns], work.at[slot], local.at[slot])

    @pl.when(active)
    def _():
        for j in range(slots):
            tile_copy(j, j).start()

    barrier = pltpu.get_barrier_semaphore()
    for d in range(CHIPS):
        for c in (0, 1):
            other = core if c == 0 else mate
            if d == 0 and c == 0:
                continue
            pl.semaphore_signal(barrier, inc=1, device_id=place(chip_at(d), other), device_id_type=MESH)

    @pl.when(r < last)
    def _():
        pl.semaphore_signal(barrier, inc=1, device_id=above, device_id_type=MESH)

    @pl.when(r > 0)
    def _():
        pl.semaphore_signal(barrier, inc=1, device_id=below, device_id_type=MESH)

    pl.semaphore_wait(barrier, 2 * CHIPS - 1 + jnp.minimum(r, 1) + jnp.minimum(last - r, 1))

    def own_send(n, where):
        return remote(panel, ag.at[p, core], ag_send.at[n], ag_recv.at[p, core], where)

    own_sends = [own_send(0, mate_at)]
    own_sends += [own_send(d, place(chip_at(d), core)) for d in (1, 3, 2)]
    for send in own_sends:
        send.start()

    def arrived(d, c):
        q = chip_at(d)
        remote(panel, ag.at[q, c], ag_send.at[0], ag_recv.at[q, c], mate_at).wait_recv()

    def pass_on(d):
        q = chip_at(d)
        return remote(ag.at[q, core], ag.at[q, core], ag_send.at[3 + d], ag_recv.at[q, core], mate_at)

    is_source = jnp.logical_and(r == owner, r < last)
    is_relay = jnp.logical_and(r > owner, r < last)

    def block_send(src, k):
        return remote(src, pg.at[k], pg_send.at[k], pg_recv.at[k], above)

    def source_send(c, own):
        @pl.when(is_source)
        def _():
            q = chip_at(OFFSETS[c])
            if c == 0:
                if own:
                    block_send(panel.at[pl.ds(part, span)], core).start()
                else:
                    block_send(ag.at[q, mate, pl.ds(part, span)], mate).start()
            else:
                for b in (0, 1):
                    block_send(ag.at[q, b, pl.ds(part, span)], 2 * c + b).start()

    def block_wait(k):
        block_send(pg.at[k], k).wait_recv()

    def relay(k):
        @pl.when(is_relay)
        def _():
            block_wait(k)
            block_send(pg.at[k], k).start()

    source_send(0, True)
    arrived(0, mate)
    source_send(0, False)

    @pl.when(active)
    def _():
        @pl.loop(0, blocks)
        def _(j):
            slot = lax.rem(j, slots)
            tile_copy(j, slot).wait()
            columns = pl.ds(pl.multiple_of(j * LANES, LANES), LANES)

            @pl.loop(0, full // TILE)
            def _(i):
                lines = pl.ds(pl.multiple_of(i * TILE, TILE), TILE)
                at = r * full + i * TILE + lax.broadcasted_iota(jnp.int32, (TILE, LANES), 0)
                to = g * span + j * LANES + lax.broadcasted_iota(jnp.int32, (TILE, LANES), 1)
                value = jnp.where(to <= at, work[slot, lines], 0.0)
                big, small = split(value)
                high[lines, columns] = big
                low[lines, columns] = small

            @pl.when(j + slots < blocks)
            def _():
                tile_copy(j + slots, slot).start()

    def mirror(c):
        @pl.when(active)
        def _():
            d = OFFSETS[c]
            q = chip_at(d)
            loads = []
            for b in (0, 1):
                if d == 0:
                    src = panel if b == 0 else ag.at[q, mate]
                    dst = core if b == 0 else mate
                else:
                    src = ag.at[q, b]
                    dst = b
                loads.append(pltpu.make_async_copy(src, work.at[dst], local.at[b]))
            for load in loads:
                load.start()
            for load in loads:
                load.wait()

            @pl.loop(0, full // TILE)
            def _(i):
                lines = pl.ds(pl.multiple_of(i * TILE, TILE), TILE)
                for b in (0, 1):
                    big, small = split(jnp.transpose(work[b, lines]))
                    pt[b * LANES:(b + 1) * LANES, lines] = big
                    pt[(2 + b) * LANES:(3 + b) * LANES, lines] = small

            @pl.loop(0, span // DEEP)
            def _(j):
                columns = pl.ds(pl.multiple_of(j * DEEP, DEEP), DEEP)
                both = dot(pt[...], high[:, columns])
                rest = dot(pt[0:2 * LANES], low[:, columns])
                value = jnp.transpose(both[:2 * LANES] + both[2 * LANES:] + rest)
                u[2 * c, columns] = value[:, :LANES]
                u[2 * c + 1, columns] = value[:, LANES:]

    def down_send(k):
        return remote(u.at[k], uin.at[k], u_send.at[k], u_recv.at[k], below)

    def home_slot():
        return uf.at[pl.ds(part, span)]

    def home_send(k):
        q = chip_at(OFFSETS[k // 2])
        return remote(u.at[k], home_slot(), u_send.at[k], uf_recv.at[g % ratio], place(q, k % 2))

    def home_copy(k):
        return pltpu.make_async_copy(u.at[k], home_slot(), uf_recv.at[g % ratio])

    is_down = r > owner
    is_home = r == owner

    def finish(k):
        @pl.when(is_down)
        def _():
            down_send(k).start()

        if k < 2:
            @pl.when(jnp.logical_and(is_home, core == k))
            def _():
                home_copy(k).start()

            @pl.when(jnp.logical_and(is_home, core != k))
            def _():
                home_send(k).start()
        else:
            @pl.when(is_home)
            def _():
                home_send(k).start()

    def add_arrived(k):
        down_send(k).wait_recv()
        load = pltpu.make_async_copy(uin.at[k], work.at[0, pl.ds(0, span)], local.at[0])
        load.start()
        load.wait()

        @pl.loop(0, span // TILE)
        def _(i):
            lines = pl.ds(pl.multiple_of(i * TILE, TILE), TILE)
            u[k, lines] = u[k, lines] + work[0, lines]

    def duty(step):
        for h in range(rows):
            k = step - h
            if h == 0:
                ks = [k for k in (2 * step, 2 * step + 1) if step < CHIPS]
            else:
                ks = [k] if 0 <= k < 2 * CHIPS else []
            for k in ks:
                @pl.when(jnp.logical_and(r == last - h, active))
                def _(k=k, h=h):
                    if h:
                        add_arrived(k)
                    finish(k)

    def trade(c):
        return remote(work.at[2 + mate], cx.at[c], cx_send.at[c], cx_recv.at[c], mate_at)

    def sum_send(c):
        d = OFFSETS[c]
        return remote(work.at[4 + c % 2], rs.at[d - 1], rs_send.at[d - 1], rs_recv.at[d - 1], place(chip_at(d), core))

    keep = pltpu.make_async_copy(work.at[4], t0, local.at[3])

    def direct(c):
        if c:
            trade(c - 1).wait_send()

        @pl.when(active)
        def _():
            q = chip_at(OFFSETS[c])

            @pl.when(r == last)
            def _():
                @pl.when(is_down)
                def _():
                    for b in (0, 1):
                        block_wait(2 * c + b)

            def load(src, b):
                return pltpu.make_async_copy(src, work.at[0, pl.ds(b * span, span)], local.at[b])

            @pl.when(is_down)
            def _():
                for b in (0, 1):
                    load(pg.at[2 * c + b], b).start()

            @pl.when(is_home)
            def _():
                for b in (0, 1):
                    if c:
                        load(ag.at[q, b, pl.ds(part, span)], b).start()
                    else:
                        @pl.when(core == b)
                        def _(b=b):
                            load(panel.at[pl.ds(part, span)], b).start()

                        @pl.when(core != b)
                        def _(b=b):
                            load(ag.at[q, b, pl.ds(part, span)], b).start()

            for b in (0, 1):
                load(pg.at[0], b).wait()

            @pl.loop(0, span // TILE)
            def _(i):
                lines = pl.ds(pl.multiple_of(i * TILE, TILE), TILE)
                for b in (0, 1):
                    big, small = split(work[0, pl.ds(pl.multiple_of(b * span + i * TILE, TILE), TILE)])
                    pgb[lines, b * LANES:(b + 1) * LANES] = big
                    pgb[lines, (2 + b) * LANES:(3 + b) * LANES] = small

            @pl.loop(0, full // TILE)
            def _(i):
                lines = pl.ds(pl.multiple_of(i * TILE, TILE), TILE)
                both = dot(high[lines], pgb[...])
                rest = dot(low[lines], pgb[:, :2 * LANES])
                value = both[:, :2 * LANES] + both[:, 2 * LANES:] + rest
                work[2, lines] = value[:, :LANES]
                work[3, lines] = value[:, LANES:]

        @pl.when(jnp.logical_not(active))
        def _():
            @pl.loop(0, full // TILE)
            def _(i):
                lines = pl.ds(pl.multiple_of(i * TILE, TILE), TILE)
                work[2, lines] = jnp.zeros((TILE, LANES), jnp.float32)
                work[3, lines] = jnp.zeros((TILE, LANES), jnp.float32)

        trade(c).start()
        trade(c).wait_recv()
        load = pltpu.make_async_copy(cx.at[c], work.at[1], local.at[2])
        load.start()
        load.wait()
        if c == 2:
            keep.wait()
        if c == 3:
            sum_send(1).wait_send()
        slot = 4 + c % 2

        @pl.loop(0, full // TILE)
        def _(i):
            lines = pl.ds(pl.multiple_of(i * TILE, TILE), TILE)
            work[slot, lines] = work[2 + core, lines] + work[1, lines]

        if c == 0:
            keep.start()
        else:
            sum_send(c).start()

    for step in range(2 * CHIPS + rows - 1):
        if step < CHIPS:
            mirror(step)
        elif step < 2 * CHIPS:
            direct(step - CHIPS)
        ready = {0: (1, 2), 2: (3,)}.get(step, ())
        for c in ready:
            arrived(OFFSETS[c], core)
            pass_on(OFFSETS[c]).start()
        for c in ready:
            arrived(OFFSETS[c], mate)
            source_send(c, True)
        if step < 2 * CHIPS - 1:
            relay(step)
        if step == 2 * CHIPS - 2:
            relay(step + 1)
        duty(step)

    trade(CHIPS - 1).wait_send()
    for c in (2, 3):
        sum_send(c).wait_send()
    for d in range(1, CHIPS):
        remote(rs.at[d - 1], rs.at[d - 1], rs_send.at[d - 1], rs_recv.at[d - 1], mate_at).wait_recv()
    for a in range(ratio):
        slot = uf.at[pl.ds(a * span, span)]
        remote(slot, slot, u_send.at[0], uf_recv.at[a], mate_at).wait_recv()
    sources = (t0, rs.at[0], rs.at[1], rs.at[2], uf)
    loads = [pltpu.make_async_copy(src, work.at[n], local.at[n]) for n, src in enumerate(sources)]
    for load in loads:
        load.start()
    for load in loads:
        load.wait()

    @pl.loop(0, full // TILE)
    def _(i):
        lines = pl.ds(pl.multiple_of(i * TILE, TILE), TILE)
        total = work[0, lines] + work[1, lines] + work[2, lines] + work[3, lines] + work[4, lines]
        work[5, lines] = total

    store = pltpu.make_async_copy(work.at[5], out, local.at[5])
    store.start()

    for send in own_sends:
        send.wait_send()
    for d in (1, 3, 2):
        pass_on(d).wait_send()

    @pl.when(jnp.logical_or(is_source, is_relay))
    def _():
        for k in range(2 * CHIPS):
            block_send(pg.at[k], k).wait_send()

    for k in range(2 * CHIPS):
        @pl.when(is_down)
        def _(k=k):
            down_send(k).wait_send()

        sent_home = jnp.logical_and(is_home, core != k) if k < 2 else is_home

        @pl.when(sent_home)
        def _(k=k):
            home_send(k).wait_send()

    store.wait()


def fused(rows, upstream, input_panel):
    full, span = upstream.shape
    width = input_panel.shape[1]
    ratio = full // span
    pieces = 2 * CHIPS
    f32 = jnp.float32
    shapes = [
        (full, width),
        (CHIPS, 2, full, width),
        (pieces, span, width),
        (pieces, span, width),
        (CHIPS - 1, full, width),
        (full, width),
        (CHIPS, full, width),
        (full, width),
    ]
    anywhere = pl.BlockSpec(memory_space=pl.ANY)
    dma = pltpu.SemaphoreType.DMA
    results = pl.pallas_call(
        functools.partial(kernel, rows),
        out_shape=[jax.ShapeDtypeStruct(shape, f32) for shape in shapes],
        in_specs=[anywhere] * 2,
        out_specs=[anywhere] * len(shapes),
        scratch_shapes=[
            pltpu.VMEM((full, span), jnp.bfloat16),
            pltpu.VMEM((full, span), jnp.bfloat16),
            pltpu.VMEM((6, full, width), f32),
            pltpu.VMEM((4 * width, full), jnp.bfloat16),
            pltpu.VMEM((span, 4 * width), jnp.bfloat16),
            pltpu.VMEM((pieces, span, width), f32),
            dma((7,)),
            dma((CHIPS, 2)),
            dma((pieces,)),
            dma((pieces,)),
            dma((pieces,)),
            dma((pieces,)),
            dma((ratio,)),
            dma((CHIPS,)),
            dma((CHIPS,)),
            dma((CHIPS - 1,)),
            dma((CHIPS - 1,)),
            dma((6,)),
        ],
        compiler_params=pltpu.CompilerParams(
            collective_id=0, has_side_effects=True, vmem_limit_bytes=67043328
        ),
    )(upstream, input_panel)
    return results[0]


def solution(mesh):
    rows = mesh.shape["row"]
    cols, reps = mesh.shape["col"], mesh.shape["rep"]
    placed = P("row", GROUP)

    def body(upstream, input_panel):
        full, span = upstream.shape
        whole_tiles = input_panel.shape[1] == LANES and full % TILE == 0 and span % TILE == 0
        if cols == 4 and reps == 2 and full == 2 * span and rows > 1 and whole_tiles:
            return fused(rows, upstream, input_panel)
        return per_device(rows, cols * reps, upstream, input_panel)

    return jax.shard_map(
        body, mesh=mesh, in_specs=(placed, placed), out_specs=placed, check_vma=False
    )
```

time: 559 us -> 384 us (0.69)
  Pallas kernels: 0 us -> 380 us
  waiting for transfers between devices: 348 us -> 0 us
  matrix products: 124 us -> 0 us
  starting transfers between devices: 28.4 us -> 0 us
  local copies, waits for them, and re-layouts: 29.7 us -> 3.05 us
  other arithmetic: 13.8 us -> 0 us
  between operations: 13.5 us -> 0.01 us
    pallas_call x0 -> x1, Pallas kernels: none -> 380 us  [fused(): pl.pallas_call(functools.partial(kernel, rows), out_shape=[jax.ShapeDtype...]
    ppermute x6 -> x0, waiting for transfers between devices: 183 us -> none  [the longest x3 95.5 us: rows_down(): lax.ppermute(total, 'row', [(r, r - 1) for r in range(rows - step, rows)])]
    all_to_all x2 -> x0, waiting for transfers between devices: 158 us -> none  [the longest x1 82.4 us: per_device(): lax.all_to_all(after(column_blocks, upper_blocks), GROUP, split_axis=0, c...]
    dot_general x2 -> x0, matrix products: 124 us -> none  [product(): lax.dot_general(left, right, (contract, ((), ())), precision=lax.Precisio...]
    ppermute x6 -> x0, starting transfers between devices: 15 us -> none  [the longest x3 9.76 us: rows_up(): lax.ppermute(held, 'row', [(r, r + 1) for r in range(step, rows - 1)])]
    add x6 -> x0, other arithmetic: 13.8 us -> none  [the longest x2 8.37 us: rows_down(): total = term if arrived is None else term + arrived]
    all_to_all x2 -> x0, starting transfers between devices: 13.4 us -> none  [the longest x1 7.36 us: per_device(): lax.all_to_all(upper_t.reshape(groups, width, col_count), GROUP, split_ax...]
    dynamic_update_slice x4 -> x0, local copies, waits for them, and re-layouts: 10.9 us -> none  [rows_up(): gathered = lax.dynamic_update_slice_in_dim(gathered, held[None], slot, 0)]
  transfers between devices with their start and end apart: 10 -> 0, of which waited for: 7 -> 0; matrix products, arithmetic and copies ran while one was open for 7% -> 0% of each run, Pallas kernels for 0% -> 0%
where the time goes in v1:
time: 384 us; the launch traced here: 383 us
  Pallas kernels  380 us (99%)
    pallas_call x1, Pallas kernels, fused(): pl.pallas_call(functools.partial(kernel, rows), out_shape=[jax.ShapeDtype...  380 us

profile of v1, /device:TPU:13, one launch (start us, length us, event | category | flops | bytes accessed | tf_op | source)
XLA Modules:
  0.0 383.0 jit_solution(14290276325239268591)
XLA Ops:
  0.0 379.9 %shard_map.28 = (f32[4096,128]{1,0:T(8,128)}, f32[4,2,4096,128]{3,2,1,0:T(8,128)}, f32[8,2048,128]{2,1,0:T(8,128)}, f32[8,2048,128]{2,1,0:T(8,128)}, f32[3,4096,...) custom-call(f32[4096,2048]{1,0:T(8,128)} %upstream.1, f32[4096,128]{1,0:T(8,128)} %panel.1), custom_call_target="tpu_custom_call" | custom-call | tf_op jit(solution)/shard_map/pallas_call | solution.py:489
  379.9 3.0 copy.4

commit v2 on v1

v2 whole, which is shorter than its diff:
```python
import functools

import jax
import jax.numpy as jnp
from jax import lax
from jax.experimental import pallas as pl
from jax.experimental.pallas import tpu as pltpu
from jax.sharding import PartitionSpec as P

GROUP = ("col", "rep")
ALL = ("row", "col", "rep")
MESH = pl.DeviceIdType.MESH
LANES = 128
CHIPS = 4
ORDER = (2, 1, 3, 0)
UPWARD = ((0, 0), (2, 0), (2, 1), (1, 0), (1, 1), (3, 0), (3, 1), (0, 1))
TILE = 512
DEEP = 256

CHUNKS = 4


def product(left, right, contract):
    return lax.dot_general(
        left,
        right,
        (contract, ((), ())),
        precision=lax.Precision.HIGH,
        preferred_element_type=jnp.float32,
    )


def per_device(rows, groups, upstream, input_panel):
    row_count, col_count = upstream.shape
    width = input_panel.shape[1]
    ratio = row_count // col_count
    row_index = lax.axis_index("row")
    col_index = lax.axis_index(GROUP)
    owner = col_index // ratio
    part = (col_index % ratio) * col_count
    rows_global = row_index * row_count + lax.broadcasted_iota(jnp.int32, (row_count, col_count), 0)
    cols_global = col_index * col_count + lax.broadcasted_iota(jnp.int32, (row_count, col_count), 1)
    lower_tile = jnp.where(cols_global <= rows_global, upstream, jnp.float32(0.0))
    panel_t = jnp.transpose(input_panel)
    step = width // CHUNKS

    def hop(value, pairs):
        return lax.ppermute(value, ALL, [(a * groups + g, b * groups + g) for a, b, g in pairs])

    outs = []
    for c in range(CHUNKS):
        band = lax.all_gather(panel_t[c * step : (c + 1) * step], GROUP, axis=0, tiled=True)
        held = lax.dynamic_slice_in_dim(band, part, col_count, 1)
        block = held
        for s in range(rows - 1):
            pairs = [(g // ratio + s, g // ratio + s + 1, g) for g in range(groups) if g // ratio + s + 1 < rows]
            held = hop(held, pairs)
            block = jnp.where(row_index == owner + s + 1, held, block)
        total = product(band, lower_tile, ((1,), (0,)))
        for s in range(rows - 1):
            r = rows - 1 - s
            pairs = [(r, r - 1, g) for g in range(groups) if g // ratio <= r - 1]
            total = total + hop(total, pairs)
        lower = product(block, lower_tile, ((1,), (1,)))
        total = jnp.where(row_index == owner, total, 0.0)
        here = lax.dynamic_slice_in_dim(lower, part, col_count, 1)
        lower = lax.dynamic_update_slice_in_dim(lower, here + total, part, 1)
        outs.append(lax.psum_scatter(lower, GROUP, scatter_dimension=0, tiled=True))
    return jnp.transpose(jnp.concatenate(outs, 0))


def split(value):
    high = value.astype(jnp.bfloat16)
    low = (value - high.astype(jnp.float32)).astype(jnp.bfloat16)
    return high, low


def dot(left, right):
    return jnp.dot(left, right, preferred_element_type=jnp.float32)


def kernel(rows, upstream, panel, out, ag, pg, uin, rs, uf, cx,
           high, low, work, pt, pgb, u,
           ag_send, ag_recv, pg_send, pg_recv, u_send, u_recv, home_sem, uf_recv,
           cx_send, cx_recv, rs_send, rs_recv, local):
    full, span = upstream.shape
    ratio = full // span
    r = lax.axis_index("row")
    col = lax.axis_index("col")
    x = lax.axis_index("rep")
    y = col // 2
    core = col % 2
    mate = 1 - core
    g = col * 2 + x
    p = 2 * y + x
    owner = g // ratio
    part = pl.multiple_of((g % ratio) * span, span)
    active = r >= owner
    last = rows - 1

    def place(chip, c):
        return {"col": 2 * (chip // 2) + c, "rep": chip % 2}

    def chip_at(d):
        across = 1 - x if d % 2 else x
        along = 1 - y if d // 2 else y
        return 2 * along + across

    def remote(src, dst, send, recv, where):
        return pltpu.make_async_remote_copy(
            src_ref=src, dst_ref=dst, send_sem=send, recv_sem=recv, device_id=where, device_id_type=MESH
        )

    mate_at = place(p, mate)
    above = {"row": jnp.minimum(r + 1, last)}
    below = {"row": jnp.maximum(r - 1, 0)}

    slots = 4
    blocks = span // LANES

    def tile_copy(j, slot):
        columns = pl.ds(pl.multiple_of(j * LANES, LANES), LANES)
        return pltpu.make_async_copy(upstream.at[:, columns], work.at[slot], local.at[slot])

    @pl.when(active)
    def _():
        for j in range(slots):
            tile_copy(j, j).start()

    barrier = pltpu.get_barrier_semaphore()
    for d in range(CHIPS):
        for c in (0, 1):
            other = core if c == 0 else mate
            if d == 0 and c == 0:
                continue
            pl.semaphore_signal(barrier, inc=1, device_id=place(chip_at(d), other), device_id_type=MESH)

    @pl.when(r < last)
    def _():
        pl.semaphore_signal(barrier, inc=1, device_id=above, device_id_type=MESH)

    @pl.when(r > 0)
    def _():
        pl.semaphore_signal(barrier, inc=1, device_id=below, device_id_type=MESH)

    pl.semaphore_wait(barrier, 2 * CHIPS - 1 + jnp.minimum(r, 1) + jnp.minimum(last - r, 1))

    def half(x_to, h):
        at = x_to if h == 0 else 1 - x_to
        return pl.ds(pl.multiple_of(at * span, span), span)

    def own_send(d, h):
        to = mate_at if d == 0 else place(chip_at(d), core)
        lines = half(to["rep"], h)
        return remote(panel.at[lines], ag.at[p, core, lines], ag_send.at[d, h], ag_recv.at[p, core, h], to)

    own_order = ((0, 0), (0, 1), (2, 0), (1, 0), (2, 1), (1, 1), (3, 0), (3, 1))
    for d, h in own_order:
        own_send(d, h).start()

    def arrived(d, c, h):
        q = chip_at(d)
        view = ag.at[q, c, half(x, h)]
        remote(view, view, ag_send.at[0, 0], ag_recv.at[q, c, h], mate_at).wait_recv()

    def pass_on(d, h):
        q = chip_at(d)
        view = ag.at[q, core, half(x, h)]
        return remote(view, view, ag_send.at[3 + d, h], ag_recv.at[q, core, h], mate_at)

    def gather(offsets, h):
        for d in offsets:
            arrived(d, core, h)
            pass_on(d, h).start()
        for d in offsets:
            arrived(d, mate, h)

    is_source = jnp.logical_and(r == owner, r < last)
    is_relay = jnp.logical_and(r > owner, r < last)

    def block_send(src, k):
        return remote(src, pg.at[k], pg_send.at[k], pg_recv.at[k], above)

    def source_send(k):
        c, b = UPWARD[k]
        q = chip_at(c)
        lines = pl.ds(part, span)

        if c:
            @pl.when(is_source)
            def _():
                block_send(ag.at[q, b, lines], k).start()
        else:
            @pl.when(jnp.logical_and(is_source, core == b))
            def _():
                block_send(panel.at[lines], k).start()

            @pl.when(jnp.logical_and(is_source, core != b))
            def _():
                block_send(ag.at[q, b, lines], k).start()

    def block_wait(k):
        block_send(pg.at[k], k).wait_recv()

    def relay(k):
        @pl.when(is_relay)
        def _():
            block_wait(k)
            block_send(pg.at[k], k).start()

    arrived(0, mate, 0)
    source_send(0)
    arrived(0, mate, 1)

    @pl.when(active)
    def _():
        @pl.loop(0, blocks)
        def _(j):
            slot = lax.rem(j, slots)
            tile_copy(j, slot).wait()
            columns = pl.ds(pl.multiple_of(j * LANES, LANES), LANES)

            @pl.loop(0, full // TILE)
            def _(i):
                lines = pl.ds(pl.multiple_of(i * TILE, TILE), TILE)
                at = r * full + i * TILE + lax.broadcasted_iota(jnp.int32, (TILE, LANES), 0)
                to = g * span + j * LANES + lax.broadcasted_iota(jnp.int32, (TILE, LANES), 1)
                value = jnp.where(to <= at, work[slot, lines], 0.0)
                big, small = split(value)
                high[lines, columns] = big
                low[lines, columns] = small

            @pl.when(j + slots < blocks)
            def _():
                tile_copy(j + slots, slot).start()

    @pl.when(jnp.logical_not(active))
    def _():
        @pl.loop(0, full // TILE)
        def _(i):
            lines = pl.ds(pl.multiple_of(i * TILE, TILE), TILE)
            work[2, lines] = jnp.zeros((TILE, LANES), jnp.float32)
            work[3, lines] = jnp.zeros((TILE, LANES), jnp.float32)

    def mirror_load(c):
        @pl.when(active)
        def _():
            d = c
            q = chip_at(d)
            loads = []
            for b in (0, 1):
                if d == 0:
                    src = panel if b == 0 else ag.at[q, mate]
                    dst = core if b == 0 else mate
                else:
                    src = ag.at[q, b]
                    dst = b
                loads.append(pltpu.make_async_copy(src, work.at[dst], local.at[b]))
            for load in loads:
                load.start()
            for load in loads:
                load.wait()

            @pl.loop(0, full // TILE)
            def _(i):
                lines = pl.ds(pl.multiple_of(i * TILE, TILE), TILE)
                for b in (0, 1):
                    big, small = split(jnp.transpose(work[b, lines]))
                    pt[b * LANES:(b + 1) * LANES, lines] = big
                    pt[(2 + b) * LANES:(3 + b) * LANES, lines] = small

    def mirror(c, h):
        @pl.when(active)
        def _():
            steps = span // DEEP // 2

            @pl.loop(h * steps, (h + 1) * steps)
            def _(j):
                columns = pl.ds(pl.multiple_of(j * DEEP, DEEP), DEEP)
                both = dot(pt[...], high[:, columns])
                rest = dot(pt[0:2 * LANES], low[:, columns])
                value = jnp.transpose(both[:2 * LANES] + both[2 * LANES:] + rest)
                lines = pl.ds(pl.multiple_of((j - h * steps) * DEEP, DEEP), DEEP)
                for b in (0, 1):
                    u[2 * c + h, b, lines] = value[:, b * LANES:(b + 1) * LANES]

    def down_send(k):
        return remote(u.at[k], uin.at[k], u_send.at[k], u_recv.at[k], below)

    def home_slot(k):
        return uf.at[pl.ds(pl.multiple_of(part + (k % 2) * (span // 2), span // 2), span // 2)]

    def home_recv(k):
        return uf_recv.at[g % ratio, k % 2]

    def home_send(k, b):
        to = place(chip_at(k // 2), b)
        return remote(u.at[k, b], home_slot(k), home_sem.at[k, b], home_recv(k), to)

    def home_copy(k, b):
        return pltpu.make_async_copy(u.at[k, b], home_slot(k), home_recv(k))

    is_down = r > owner
    is_home = r == owner

    def finish(k):
        @pl.when(is_down)
        def _():
            down_send(k).start()

        for b in (0, 1):
            if k // 2:
                @pl.when(is_home)
                def _(b=b):
                    home_send(k, b).start()
            else:
                @pl.when(jnp.logical_and(is_home, core == b))
                def _(b=b):
                    home_copy(k, b).start()

                @pl.when(jnp.logical_and(is_home, core != b))
                def _(b=b):
                    home_send(k, b).start()

    def add_arrived(k):
        down_send(k).wait_recv()
        loads = [
            pltpu.make_async_copy(uin.at[k, b], work.at[0, pl.ds(b * (span // 2), span // 2)], local.at[b])
            for b in (0, 1)
        ]
        for load in loads:
            load.start()
        for load in loads:
            load.wait()

        @pl.loop(0, span // 2 // TILE)
        def _(i):
            for b in (0, 1):
                lines = pl.ds(pl.multiple_of(i * TILE, TILE), TILE)
                other = pl.ds(pl.multiple_of(b * (span // 2) + i * TILE, TILE), TILE)
                u[k, b, lines] = u[k, b, lines] + work[0, other]

    def relay_slot(row, k):
        if row == 1:
            return (0, 2, 3, 5, 6, 7, 8, 9)[k]
        return min((2, 4, 6, 8, 10, 12, 13, 14)[k] + 2 * (row - 2), (7, 7, 7, 11, 11, 13, 13, 15)[k])

    def duty_slot(h, k):
        if h == 0:
            return (1, 2, 4, 5, 6, 7, 10, 11)[k]
        if h == 1:
            return (3, 5, 7, 9, 11, 13, 14, 16)[k]
        return (5, 7, 9, 11, 14, 15, 17, 18)[k] if h == 2 else (7, 9, 11, 12, 15, 16, 18, 19)[k] + h - 3

    def service(slot):
        for k in range(2 * CHIPS):
            if duty_slot(0, k) == slot:
                @pl.when(r == last)
                def _(k=k):
                    finish(k)
        if slot == 1:
            gather((1, 2), 0)
            for k in (1, 2, 3, 4):
                source_send(k)
        if slot == 5:
            gather((3,), 0)
            for k in (5, 6, 7):
                source_send(k)
        for h in range(1, rows):
            for k in range(2 * CHIPS):
                if duty_slot(h, k) == slot:
                    @pl.when(jnp.logical_and(r == last - h, active))
                    def _(k=k):
                        add_arrived(k)
                        finish(k)
        for row in range(1, last):
            for k in range(2 * CHIPS):
                if relay_slot(row, k) == slot:
                    @pl.when(r == row)
                    def _(k=k):
                        relay(k)
        if slot == 2:
            gather((1, 2), 1)
        if slot == 7:
            gather((3,), 1)

    def rows_half(h):
        return pl.ds(h * (full // 2), full // 2)

    def trade(c, h):
        lines = rows_half(h)
        return remote(work.at[2 + mate, lines], cx.at[c, lines], cx_send.at[c, h], cx_recv.at[c, h], mate_at)

    def sum_send(c, h):
        d = c
        lines = rows_half(h)
        return remote(
            work.at[4 + ORDER.index(c) % 2, lines], rs.at[d - 1, lines],
            rs_send.at[d - 1, h], rs_recv.at[d - 1, h], place(chip_at(d), core),
        )

    def direct_load(t):
        c = ORDER[t]

        @pl.when(active)
        def _():
            q = chip_at(c)

            @pl.when(jnp.logical_and(r == last, is_down))
            def _():
                for k in range(2 * CHIPS):
                    if UPWARD[k][0] == c:
                        block_wait(k)

            def load(src, b):
                return pltpu.make_async_copy(src, work.at[0, pl.ds(b * span, span)], local.at[b])

            @pl.when(is_down)
            def _():
                for b in (0, 1):
                    load(pg.at[UPWARD.index((c, b))], b).start()

            @pl.when(is_home)
            def _():
                for b in (0, 1):
                    if c:
                        load(ag.at[q, b, pl.ds(part, span)], b).start()
                    else:
                        @pl.when(core == b)
                        def _(b=b):
                            load(panel.at[pl.ds(part, span)], b).start()

                        @pl.when(core != b)
                        def _(b=b):
                            load(ag.at[q, b, pl.ds(part, span)], b).start()

            for b in (0, 1):
                load(pg.at[0], b).wait()

            @pl.loop(0, span // TILE)
            def _(i):
                lines = pl.ds(pl.multiple_of(i * TILE, TILE), TILE)
                for b in (0, 1):
                    big, small = split(work[0, pl.ds(pl.multiple_of(b * span + i * TILE, TILE), TILE)])
                    pgb[lines, b * LANES:(b + 1) * LANES] = big
                    pgb[lines, (2 + b) * LANES:(3 + b) * LANES] = small

        if t:
            for h in (0, 1):
                trade(ORDER[t - 1], h).wait_send()

    def direct(c, h):
        @pl.when(active)
        def _():
            steps = full // TILE // 2

            @pl.loop(h * steps, (h + 1) * steps)
            def _(i):
                lines = pl.ds(pl.multiple_of(i * TILE, TILE), TILE)
                both = dot(high[lines], pgb[...])
                rest = dot(low[lines], pgb[:, :2 * LANES])
                value = both[:, :2 * LANES] + both[:, 2 * LANES:] + rest
                work[2, lines] = value[:, :LANES]
                work[3, lines] = value[:, LANES:]

        trade(c, h).start()

    def direct_sum(t):
        c = ORDER[t]
        slot = 4 + t % 2 if c else 2 + core
        for h in (0, 1):
            if t == 2:
                sum_send(ORDER[0], h).wait_send()
            trade(c, h).wait_recv()
            load = pltpu.make_async_copy(cx.at[c, rows_half(h)], work.at[1, rows_half(h)], local.at[2])
            load.start()
            load.wait()
            steps = full // TILE // 2

            @pl.loop(h * steps, (h + 1) * steps)
            def _(i):
                lines = pl.ds(pl.multiple_of(i * TILE, TILE), TILE)
                work[slot, lines] = work[2 + core, lines] + work[1, lines]

            if c:
                sum_send(c, h).start()

    service(0)
    tasks = (("m", 0), ("m", 1), ("m", 2), ("d", 0), ("m", 3), ("d", 1), ("d", 2), ("d", 3))
    for i, (kind, n) in enumerate(tasks):
        if kind == "m":
            mirror_load(n)
        else:
            direct_load(n)
        for h in (0, 1):
            if kind == "m":
                mirror(n, h)
            else:
                c = ORDER[n]
                direct(c, h)
                if h:
                    direct_sum(n)
            service(2 * i + h + (2 if i else 1))
        if i == 0:
            service(3)
    for slot in range(4 * CHIPS + 2, 4 * CHIPS + 2 + rows):
        service(slot)

    def add_up(sources):
        loads = [pltpu.make_async_copy(src, work.at[n], local.at[n]) for n, src in enumerate(sources)]
        for load in loads:
            load.start()
        for load in loads:
            load.wait()

        @pl.loop(0, full // TILE)
        def _(i):
            lines = pl.ds(pl.multiple_of(i * TILE, TILE), TILE)
            total = work[2 + core, lines]
            for n in range(len(sources)):
                total = total + work[n, lines]
            work[2 + core, lines] = total

    def sum_wait(d):
        for h in (0, 1):
            view = rs.at[d - 1, rows_half(h)]
            remote(view, view, rs_send.at[d - 1, h], rs_recv.at[d - 1, h], mate_at).wait_recv()

    for h in (0, 1):
        trade(ORDER[-1], h).wait_send()
    sum_wait(1)
    sum_wait(2)
    add_up((rs.at[0], rs.at[1]))
    sum_wait(3)
    add_up((rs.at[2],))
    for a in range(ratio):
        for h in (0, 1):
            view = uf.at[pl.ds(a * span + h * (span // 2), span // 2)]
            remote(view, view, home_sem.at[0, 0], uf_recv.at[a, h], mate_at).wait_recv()
    add_up((uf,))
    store = pltpu.make_async_copy(work.at[2 + core], out, local.at[5])
    store.start()

    for d, h in own_order:
        own_send(d, h).wait_send()
    for d in (1, 2, 3):
        for h in (0, 1):
            pass_on(d, h).wait_send()
    for h in (0, 1):
        sum_send(ORDER[1], h).wait_send()
        sum_send(ORDER[2], h).wait_send()

    @pl.when(jnp.logical_or(is_source, is_relay))
    def _():
        for k in range(2 * CHIPS):
            block_send(pg.at[k], k).wait_send()

    for k in range(2 * CHIPS):
        @pl.when(is_down)
        def _(k=k):
            down_send(k).wait_send()

        for b in (0, 1):
            sent_home = is_home if k // 2 else jnp.logical_and(is_home, core != b)

            @pl.when(sent_home)
            def _(k=k, b=b):
                home_send(k, b).wait_send()

    store.wait()


def fused(rows, upstream, input_panel):
    full, span = upstream.shape
    width = input_panel.shape[1]
    ratio = full // span
    pieces = 2 * CHIPS
    f32 = jnp.float32
    shapes = [
        (full, width),
        (CHIPS, 2, full, width),
        (pieces, span, width),
        (pieces, 2, span // 2, width),
        (CHIPS - 1, full, width),
        (full, width),
        (CHIPS, full, width),
    ]
    anywhere = pl.BlockSpec(memory_space=pl.ANY)
    dma = pltpu.SemaphoreType.DMA
    results = pl.pallas_call(
        functools.partial(kernel, rows),
        out_shape=[jax.ShapeDtypeStruct(shape, f32) for shape in shapes],
        in_specs=[anywhere] * 2,
        out_specs=[anywhere] * len(shapes),
        scratch_shapes=[
            pltpu.VMEM((full, span), jnp.bfloat16),
            pltpu.VMEM((full, span), jnp.bfloat16),
            pltpu.VMEM((6, full, width), f32),
            pltpu.VMEM((4 * width, full), jnp.bfloat16),
            pltpu.VMEM((span, 4 * width), jnp.bfloat16),
            pltpu.VMEM((pieces, 2, span // 2, width), f32),
            dma((7, 2)),
            dma((CHIPS, 2, 2)),
            dma((pieces,)),
            dma((pieces,)),
            dma((pieces,)),
            dma((pieces,)),
            dma((pieces, 2)),
            dma((ratio, 2)),
            dma((CHIPS, 2)),
            dma((CHIPS, 2)),
            dma((CHIPS - 1, 2)),
            dma((CHIPS - 1, 2)),
            dma((6,)),
        ],
        compiler_params=pltpu.CompilerParams(
            collective_id=0, has_side_effects=True, vmem_limit_bytes=67043328
        ),
    )(upstream, input_panel)
    return results[0]


def solution(mesh):
    rows = mesh.shape["row"]
    cols, reps = mesh.shape["col"], mesh.shape["rep"]
    placed = P("row", GROUP)

    def body(upstream, input_panel):
        full, span = upstream.shape
        whole_tiles = input_panel.shape[1] == LANES and full % TILE == 0 and span % (2 * TILE) == 0
        if cols == 4 and reps == 2 and full == 2 * span and rows > 1 and whole_tiles:
            return fused(rows, upstream, input_panel)
        return per_device(rows, cols * reps, upstream, input_panel)

    return jax.shard_map(
        body, mesh=mesh, in_specs=(placed, placed), out_specs=placed, check_vma=False
    )
```

time: 384 us -> 299 us (0.78)
  the two profiles are of different devices: /device:TPU:13 before, /device:TPU:5 now
where the time goes in v2:
time: 299 us; the launch traced here: 298 us
  Pallas kernels  295 us (99%)
  local copies, waits for them, and re-layouts  3.05 us (1%)
    pallas_call x1, Pallas kernels, fused(): pl.pallas_call(functools.partial(kernel, rows), out_shape=[jax.ShapeDtype...  295 us

profile of v2, /device:TPU:5, one launch (start us, length us, event | category | flops | bytes accessed | tf_op | source)
XLA Modules:
  0.0 298.5 jit_solution(12409756586379531904)
XLA Ops:
  0.0 295.4 %shard_map.28 = (f32[4096,128]{1,0:T(8,128)}, f32[4,2,4096,128]{3,2,1,0:T(8,128)}, f32[8,2048,128]{2,1,0:T(8,128)}, f32[8,2,1024,128]{3,2,1,0:T(8,128)}, f32[3,4...) custom-call(f32[4096,2048]{1,0:T(8,128)} %upstream.1, f32[4096,128]{1,0:T(8,128)} %panel.1), custom_call_target="tpu_custom_call" | custom-call | tf_op jit(solution)/shard_map/pallas_call | solution.py:590
  295.4 3.0 %copy.4 = f32[4096,128]{1,0:T(8,128)} copy(f32[4096,128]{1,0:T(8,128)} %get-tuple-element.6) | data formatting | bytes 4194304

commit v3 on v2

--- a/solution.py
+++ b/solution.py
@@ -102,8 +102,8 @@
         return {"col": 2 * (chip // 2) + c, "rep": chip % 2}
 
     def chip_at(d):
-        across = 1 - x if d % 2 else x
-        along = 1 - y if d // 2 else y
+        across = x + (d % 2) * (1 - 2 * x)
+        along = y + (d // 2) * (1 - 2 * y)
         return 2 * along + across
 
     def remote(src, dst, send, recv, where):
@@ -249,7 +249,7 @@
             q = chip_at(d)
             loads = []
             for b in (0, 1):
-                if d == 0:
+                if isinstance(d, int) and d == 0:
                     src = panel if b == 0 else ag.at[q, mate]
                     dst = core if b == 0 else mate
                 else:
@@ -284,8 +284,8 @@
                 for b in (0, 1):
                     u[2 * c + h, b, lines] = value[:, b * LANES:(b + 1) * LANES]
 
-    def down_send(k):
-        return remote(u.at[k], uin.at[k], u_send.at[k], u_recv.at[k], below)
+    def down_send(k, b):
+        return remote(u.at[k, b], uin.at[k, b], u_send.at[k, b], u_recv.at[k, b], below)
 
     def home_slot(k):
         return uf.at[pl.ds(pl.multiple_of(part + (k % 2) * (span // 2), span // 2), span // 2)]
@@ -303,42 +303,36 @@
     is_down = r > owner
     is_home = r == owner
 
-    def finish(k):
+    def finish(k, b):
         @pl.when(is_down)
         def _():
-            down_send(k).start()
-
-        for b in (0, 1):
-            if k // 2:
-                @pl.when(is_home)
-                def _(b=b):
-                    home_send(k, b).start()
-            else:
-                @pl.when(jnp.logical_and(is_home, core == b))
-                def _(b=b):
-                    home_copy(k, b).start()
-
-                @pl.when(jnp.logical_and(is_home, core != b))
-                def _(b=b):
-                    home_send(k, b).start()
-
-    def add_arrived(k):
-        down_send(k).wait_recv()
-        loads = [
-            pltpu.make_async_copy(uin.at[k, b], work.at[0, pl.ds(b * (span // 2), span // 2)], local.at[b])
-            for b in (0, 1)
-        ]
-        for load in loads:
-            load.start()
-        for load in loads:
-            load.wait()
+            down_send(k, b).start()
+
+        if k // 2:
+            @pl.when(is_home)
+            def _():
+                home_send(k, b).start()
+        else:
+            @pl.when(jnp.logical_and(is_home, core == b))
+            def _():
+                home_copy(k, b).start()
+
+            @pl.when(jnp.logical_and(is_home, core != b))
+            def _():
+                home_send(k, b).start()
+
+    def add_arrived(k, b):
+        down_send(k, b).wait_recv()
+        lines = pl.ds(b * (span // 2), span // 2)
+        load = pltpu.make_async_copy(uin.at[k, b], work.at[0, lines], local.at[b])
+        load.start()
+        load.wait()
 
         @pl.loop(0, span // 2 // TILE)
         def _(i):
-            for b in (0, 1):
-                lines = pl.ds(pl.multiple_of(i * TILE, TILE), TILE)
-                other = pl.ds(pl.multiple_of(b * (span // 2) + i * TILE, TILE), TILE)
-                u[k, b, lines] = u[k, b, lines] + work[0, other]
+            lines = pl.ds(pl.multiple_of(i * TILE, TILE), TILE)
+            other = pl.ds(pl.multiple_of(b * (span // 2) + i * TILE, TILE), TILE)
+            u[k, b, lines] = u[k, b, lines] + work[0, other]
 
     def relay_slot(row, k):
         if row == 1:
@@ -357,7 +351,8 @@
             if duty_slot(0, k) == slot:
                 @pl.when(r == last)
                 def _(k=k):
-                    finish(k)
+                    for b in (0, 1):
+                        finish(k, b)
         if slot == 1:
             gather((1, 2), 0)
             for k in (1, 2, 3, 4):
@@ -371,8 +366,9 @@
                 if duty_slot(h, k) == slot:
                     @pl.when(jnp.logical_and(r == last - h, active))
                     def _(k=k):
-                        add_arrived(k)
-                        finish(k)
+                        for b in (0, 1):
+                            add_arrived(k, b)
+                            finish(k, b)
         for row in range(1, last):
             for k in range(2 * CHIPS):
                 if relay_slot(row, k) == slot:
@@ -391,16 +387,21 @@
         lines = rows_half(h)
         return remote(work.at[2 + mate, lines], cx.at[c, lines], cx_send.at[c, h], cx_recv.at[c, h], mate_at)
 
-    def sum_send(c, h):
-        d = c
+    def chunk_of(t):
+        return ORDER[t] if isinstance(t, int) else 2 - t + 3 * (t // 2)
+
+    def sum_send(t, h):
+        d = chunk_of(t)
         lines = rows_half(h)
         return remote(
-            work.at[4 + ORDER.index(c) % 2, lines], rs.at[d - 1, lines],
+            work.at[4 + t % 2, lines], rs.at[d - 1, lines],
             rs_send.at[d - 1, h], rs_recv.at[d - 1, h], place(chip_at(d), core),
         )
 
     def direct_load(t):
-        c = ORDER[t]
+        c = chunk_of(t)
+        own = isinstance(t, int) and c == 0
+        at = [UPWARD.index((c, b)) if isinstance(t, int) else 1 + 2 * t + b for b in (0, 1)]
 
         @pl.when(active)
         def _():
@@ -408,9 +409,8 @@
 
             @pl.when(jnp.logical_and(r == last, is_down))
             def _():
-                for k in range(2 * CHIPS):
-                    if UPWARD[k][0] == c:
-                        block_wait(k)
+                for b in (0, 1):
+                    block_wait(at[b])
 
             def load(src, b):
                 return pltpu.make_async_copy(src, work.at[0, pl.ds(b * span, span)], local.at[b])
@@ -418,12 +418,12 @@
             @pl.when(is_down)
             def _():
                 for b in (0, 1):
-                    load(pg.at[UPWARD.index((c, b))], b).start()
+                    load(pg.at[at[b]], b).start()
 
             @pl.when(is_home)
             def _():
                 for b in (0, 1):
-                    if c:
+                    if not own:
                         load(ag.at[q, b, pl.ds(part, span)], b).start()
                     else:
                         @pl.when(core == b)
@@ -445,16 +445,12 @@
                     pgb[lines, b * LANES:(b + 1) * LANES] = big
                     pgb[lines, (2 + b) * LANES:(3 + b) * LANES] = small
 
-        if t:
-            for h in (0, 1):
-                trade(ORDER[t - 1], h).wait_send()
-
-    def direct(c, h):
+    def direct(c, h, begin=0, end=2):
         @pl.when(active)
         def _():
-            steps = full // TILE // 2
-
-            @pl.loop(h * steps, (h + 1) * steps)
+            steps = full // TILE // 4
+
+            @pl.loop((2 * h + begin) * steps, (2 * h + end) * steps)
             def _(i):
                 lines = pl.ds(pl.multiple_of(i * TILE, TILE), TILE)
                 both = dot(high[lines], pgb[...])
@@ -463,46 +459,101 @@
                 work[2, lines] = value[:, :LANES]
                 work[3, lines] = value[:, LANES:]
 
-        trade(c, h).start()
-
-    def direct_sum(t):
-        c = ORDER[t]
-        slot = 4 + t % 2 if c else 2 + core
-        for h in (0, 1):
-            if t == 2:
-                sum_send(ORDER[0], h).wait_send()
-            trade(c, h).wait_recv()
-            load = pltpu.make_async_copy(cx.at[c, rows_half(h)], work.at[1, rows_half(h)], local.at[2])
-            load.start()
-            load.wait()
-            steps = full // TILE // 2
-
-            @pl.loop(h * steps, (h + 1) * steps)
-            def _(i):
-                lines = pl.ds(pl.multiple_of(i * TILE, TILE), TILE)
-                work[slot, lines] = work[2 + core, lines] + work[1, lines]
-
-            if c:
-                sum_send(c, h).start()
+        if end == 2:
+            trade(c, h).start()
+
+    def direct_sum(t, h):
+        c = chunk_of(t)
+        own = isinstance(t, int) and c == 0
+        slot = 2 + core if own else 4 + t % 2
+        if not own:
+            @pl.when(t == 2)
+            def _():
+                sum_send(0, h).wait_send()
+
+        trade(c, h).wait_recv()
+        load = pltpu.make_async_copy(cx.at[c, rows_half(h)], work.at[1, rows_half(h)], local.at[2])
+        load.start()
+        load.wait()
+        steps = full // TILE // 2
+
+        @pl.loop(h * steps, (h + 1) * steps)
+        def _(i):
+            lines = pl.ds(pl.multiple_of(i * TILE, TILE), TILE)
+            work[slot, lines] = work[2 + core, lines] + work[1, lines]
+
+        if not own:
+            sum_send(t, h).start()
+        trade(c, h).wait_send()
+
+    def direct_rest(t):
+        direct(chunk_of(t), 1, 0, 1)
+        direct_sum(t, 0)
+        direct(chunk_of(t), 1, 1, 2)
+        direct_sum(t, 1)
+
+    def mirror_task(n, during, after):
+        mirror_load(n)
+        mirror(n, 0)
+        during()
+        mirror(n, 1)
+        after()
+
+    def direct_task(n, during, after):
+        direct_load(n)
+        direct(chunk_of(n), 0)
+        during()
+        direct_rest(n)
+        after()
+
+    def at_slot(slot):
+        return functools.partial(service, slot)
 
     service(0)
-    tasks = (("m", 0), ("m", 1), ("m", 2), ("d", 0), ("m", 3), ("d", 1), ("d", 2), ("d", 3))
-    for i, (kind, n) in enumerate(tasks):
-        if kind == "m":
+    mirror_task(0, at_slot(1), at_slot(2))
+    service(3)
+    mirror_task(1, at_slot(4), at_slot(5))
+
+    lower = r < last - 1
+
+    @pl.loop(2, 7)
+    def _(i):
+        def within(first):
+            def run():
+                for n in range(2, 7):
+                    @pl.when(i == n)
+                    def _(n=n):
+                        service(2 * n + first)
+            return run
+
+        turn = jnp.where(lower, i >= 5, jnp.logical_and(i % 2 == 0, i < 5))
+        n = jnp.where(lower, i - 3, 1 + i // 2)
+
+        @pl.when(turn)
+        def _():
             mirror_load(n)
-        else:
-            direct_load(n)
-        for h in (0, 1):
-            if kind == "m":
-                mirror(n, h)
-            else:
-                c = ORDER[n]
-                direct(c, h)
-                if h:
-                    direct_sum(n)
-            service(2 * i + h + (2 if i else 1))
-        if i == 0:
-            service(3)
+            mirror(n, 0)
+
+        t = jnp.where(lower, i - 2, (i - 2) // 2)
+
+        @pl.when(jnp.logical_not(turn))
+        def _():
+            direct_load(t)
+            direct(chunk_of(t), 0)
+
+        within(2)()
+
+        @pl.when(turn)
+        def _():
+            mirror(n, 1)
+
+        @pl.when(jnp.logical_not(turn))
+        def _():
+            direct_rest(t)
+
+        within(3)()
+
+    direct_task(3, at_slot(16), at_slot(17))
     for slot in range(4 * CHIPS + 2, 4 * CHIPS + 2 + rows):
         service(slot)
 
@@ -526,8 +577,6 @@
             view = rs.at[d - 1, rows_half(h)]
             remote(view, view, rs_send.at[d - 1, h], rs_recv.at[d - 1, h], mate_at).wait_recv()
 
-    for h in (0, 1):
-        trade(ORDER[-1], h).wait_send()
     sum_wait(1)
     sum_wait(2)
     add_up((rs.at[0], rs.at[1]))
@@ -547,8 +596,8 @@
         for h in (0, 1):
             pass_on(d, h).wait_send()
     for h in (0, 1):
-        sum_send(ORDER[1], h).wait_send()
-        sum_send(ORDER[2], h).wait_send()
+        sum_send(1, h).wait_send()
+        sum_send(2, h).wait_send()
 
     @pl.when(jnp.logical_or(is_source, is_relay))
     def _():
@@ -558,7 +607,8 @@
     for k in range(2 * CHIPS):
         @pl.when(is_down)
         def _(k=k):
-            down_send(k).wait_send()
+            for b in (0, 1):
+                down_send(k, b).wait_send()
 
         for b in (0, 1):
             sent_home = is_home if k // 2 else jnp.logical_and(is_home, core != b)
@@ -603,8 +653,8 @@
             dma((CHIPS, 2, 2)),
             dma((pieces,)),
             dma((pieces,)),
-            dma((pieces,)),
-            dma((pieces,)),
+            dma((pieces, 2)),
+            dma((pieces, 2)),
             dma((pieces, 2)),
             dma((ratio, 2)),
             dma((CHIPS, 2)),

time: 299 us -> 283 us (0.946)
  the two profiles are of different devices: /device:TPU:5 before, /device:TPU:13 now
where the time goes in v3:
time: 283 us; the launch traced here: 278 us
  Pallas kernels  275 us (97%)
  local copies, waits for them, and re-layouts  3.05 us (1%)
    pallas_call x1, Pallas kernels, fused(): pl.pallas_call(functools.partial(kernel, rows), out_shape=[jax.ShapeDtype...  275 us

profile of v3, /device:TPU:13, one launch (start us, length us, event | category | flops | bytes accessed | tf_op | source)
XLA Modules:
  0.0 278.3 jit_solution(7174162006456734457)
XLA Ops:
  0.0 275.3 %shard_map.28 = (f32[4096,128]{1,0:T(8,128)}, f32[4,2,4096,128]{3,2,1,0:T(8,128)}, f32[8,2048,128]{2,1,0:T(8,128)}, f32[8,2,1024,128]{3,2,1,0:T(8,128)}, f32[3,4...) custom-call(f32[4096,2048]{1,0:T(8,128)} %upstream.1, f32[4096,128]{1,0:T(8,128)} %panel.1), custom_call_target="tpu_custom_call" | custom-call | tf_op jit(solution)/shard_map/pallas_call | solution.py:640
  275.3 3.0 %copy.4 = f32[4096,128]{1,0:T(8,128)} copy(f32[4096,128]{1,0:T(8,128)} %get-tuple-element.6) | data formatting | bytes 4194304
